TPU v7x, 32 devices: a whole 2x2x4 slice. The times are simulated.
32 devices in a mesh: dp: 4 (over y, x), tp: 8 (over z, core).
Axes of the slice: x: 2, y: 2, z: 4, core: 2. Of those that a mesh axis runs over, the one named last changes fastest.
Arguments:
- gradients: bfloat16 [4, 4, 3072, 768], P('dp', None, 'tp'), may hold values from -6 to 6, as said below
- right_factor: float32 [4, 768, 8], replicated, may hold values from -6 to 6
- weights_before: float32 [4, 3072, 768], P(None, 'tp', 'dp'), may hold values from -0.21875 to 0.21875
- momentum: float32 [4, 3072, 768], P(None, 'tp', 'dp'), may hold values from -0.3125 to 0.3125
Outputs:
- new_weights: float32 [4, 3072, 768], P(None, 'tp', 'dp')
- new_basis: float32 [4, 768, 8], replicated
- new_momentum: float32 [4, 3072, 768], P(None, 'tp', 'dp')
Inputs may be any that keep to these rules, and one draw needn't show every extreme that they name: gradients holds numbers from -6 to 6.
All inputs are finite; a program needn't handle non-finite values.
Results may differ from a plain program's by a relative error of at most 0.0003.
Values sent between devices are 32-bit elements.
A program may use at most 64 MiB of HBM per device.

v0:
```python
import jax
import jax.numpy as jnp
from jax import lax
from jax.sharding import PartitionSpec as P

RANK = 8


def on_device(gradients, right_factor, weights_before, momentum):
    own_grads = gradients[0]
    part_left = jnp.einsum(
        "liw,lwr->lir",
        own_grads,
        right_factor.astype(jnp.bfloat16),
        preferred_element_type=jnp.float32,
    )
    left = lax.psum(part_left, "dp")
    part_gram = jnp.einsum("lir,lis->lrs", left, left, precision=lax.Precision.HIGHEST)
    small_left = left.astype(jnp.bfloat16)
    part_right = jnp.einsum(
        "liw,lir->lwr", own_grads, small_left, preferred_element_type=jnp.float32
    )
    own_share = part_gram / lax.axis_size("dp")
    right, gram = lax.psum((part_right, own_share), ("dp", "tp"))
    gram = gram + 0.001 * jnp.mean(jnp.diagonal(gram, axis1=1, axis2=2), axis=1)[
        :, None, None
    ] * jnp.eye(RANK, dtype=jnp.float32)
    place = lax.axis_index("dp") * weights_before.shape[2]
    own_right = lax.dynamic_slice_in_dim(right, place, weights_before.shape[2], axis=1)
    root = jnp.linalg.cholesky(gram)
    half = lax.linalg.triangular_solve(
        root, jnp.swapaxes(own_right, 1, 2), left_side=True, lower=True
    )
    mixed = lax.linalg.triangular_solve(root, half, left_side=True, lower=True, transpose_a=True)
    change = jnp.einsum(
        "lir,lrw->liw", left, mixed, precision=lax.Precision.HIGHEST
    ) / lax.axis_size("dp")
    new_momentum = 0.9 * momentum + change
    new_weights = weights_before - 0.02 * new_momentum
    new_basis = right * lax.rsqrt(jnp.mean(right * right, axis=(1, 2), keepdims=True) + 1e-12)
    return (new_weights, new_basis, new_momentum)


def solution(mesh):
    in_specs = (P("dp", None, "tp", None), P(), P(None, "tp", "dp"), P(None, "tp", "dp"))
    out_specs = (P(None, "tp", "dp"), P(), P(None, "tp", "dp"))
    return jax.shard_map(
        on_device, mesh=mesh, in_specs=in_specs, out_specs=out_specs, check_vma=False
    )
```

profile of v0, /device:TPU:8, one launch (start us, length us, event | category | flops | bytes accessed | tf_op | source)
XLA Modules:
  0.0 166.5 jit_solution(5481928536512770521)
XLA Ops:
  7.2 0.0 copy-start
  7.2 0.0 all-reduce.2.cloned.1.call-start
  7.2 1.6 copy-done
  8.8 1.6 fusion.2
  10.4 16.7 %psum.21 = f32[4,384,8]{1,2,0:T(8,128)S(1)} all-reduce(f32[4,384,8]{1,2,0:T(8,128)S(1)} %fusion.2), channel_id=1, replica_groups=mesh['dp'=4,'tp'=8] {'dp'}, use_global_device_ids=true, to_apply=%region_0.0 | all-reduce | flops 12288 | bytes 98304 | tf_op jit(solution)/shard_map/psum | solution.py:17
  27.1 1.1 fusion.5
  28.2 0.0 all-reduce.2.cloned.1.call-update
  28.3 0.2 convolution_multiply_fusion.1
  28.5 0.1 copy.13
  28.5 39.5 %psum.22 = f32[4,8,8]{1,2,0:T(8,128)S(1)} all-reduce(f32[4,8,8]{1,2,0:T(8,128)S(1)} %convolution_multiply_fusion.1), channel_id=1, replica_groups=mesh['dp'=4,'tp'=8] {'dp','tp'}, use_global_device_ids=true, to_apply=%region_1.0 | all-reduce | flops 256 | bytes 2048 | tf_op jit(solution)/shard_map/psum | solution.py:24
  68.0 0.1 copy.12
  68.1 0.6 gather_fusion
  68.7 0.1 multiply_add_fusion
  68.8 0.1 copy.14
  68.9 0.1 fusion.15
  69.0 2.9 %custom-call.9 = f32[4,8,8]{2,1,0:T(8,128)S(1)} custom-call(f32[4,8,8]{2,1,0:T(8,128)S(1)} %fusion.15), custom_call_target="Cholesky" | custom-call | tf_op jit(solution)/shard_map/jit(cholesky)/cholesky | solution.py:30
  71.9 0.1 select_reduce_fusion
  71.9 0.1 compare_reduce_fusion
  72.0 0.1 select_bitcast_fusion
  72.1 2.5 %custom-call.10 = f32[4,1,8,8]{2,3,1,0:T(8,128)S(1)} custom-call(f32[4,1,8,8]{3,2,1,0:T(8,128)S(1)} %select_bitcast_fusion), custom_call_target="InvertDiagBlocksLowerTriangular" | custom-call | tf_op jit(solution)/shard_map/triangular_solve | solution.py:34
  74.6 77.7 %all-reduce.2.cloned.1.call-done = f32[4,768,8]{1,2,0:T(8,128)} async-done(((f32[4,768,8]{1,2,0:T(8,128)}), f32[4,768,8]{1,2,0:T(8,128)}) %all-reduce.2.cloned.1.call-update) | async-done | bytes 98320 | tf_op jit(solution)/shard_map/psum | solution.py:24
  152.3 1.0 multiply_reduce_fusion
  153.3 1.1 fusion.9
  154.4 0.2 fusion.12
  154.5 0.0 copy-start.1
  154.5 4.4 %multiply_subtract_fusion = (f32[4,384,192]{1,2,0:T(8,128)}, f32[4,384,192]{1,2,0:T(8,128)}) fusion(f32[4,384,192]{1,2,0:T(8,128)} %param.6, f32[4,384,8]{1,2,0:T(8,128)S(1)} %psum.21, f32[4,8,192]{2,1,0:T(8,128)S(1)} %fusion.12, f32[4,384,192]{1,2,0:T(8,128)} %param.7), kind=kOutput, calls=%fused_computation.7 | convolution fusion | flops 29786112 | bytes 4792320 | tf_op jit(solution)/shard_map/lir,lrw->liw/dot_general | solution.py:35
  158.9 0.0 copy-done.1
  158.9 0.7 broadcast_multiply_fusion
  (7 shorter events, 0.1 us)
Async XLA Ops:
  7.2 1.7 %copy-start = (bf16[1,4,384,768]{3,2,1,0:T(8,128)(2,1)S(1)}, bf16[1,4,384,768]{3,2,1,0:T(8,128)(2,1)}, u32[]{:S(2)}) copy-start(bf16[1,4,384,768]{3,2,1,0:T(8,128)(2,1)} %param.4) | copy-start | bytes 7077892
  7.2 145.1 %all-reduce.2.cloned.1.call-start = ((), (), s32[]{:S(2)}) async-start(), calls=%async_computation | async-start | bytes 196608 | tf_op jit(solution)/shard_map/psum | solution.py:24
  154.5 4.4 %copy-start.1 = (f32[4,768,8]{1,2,0:T(8,128)S(1)}, f32[4,768,8]{1,2,0:T(8,128)}, u32[]{:S(2)}) copy-start(f32[4,768,8]{1,2,0:T(8,128)} %all-reduce.2.cloned.1.call-done) | copy-start | bytes 294916
Sparse Core Ops, SparseCore 0:
  28.3 123.8 all-reduce.1
where the time goes:
time: 167 us; the launch traced here: 166 us
  waiting for transfers between devices  77.7 us (47%)
  blocking collectives  56.2 us (34%)
  between operations  14.1 us (8%)
  matrix products  8.45 us (5%)
  other arithmetic  7.59 us (5%)
  local copies, waits for them, and re-layouts  2.47 us (1%)
    psum x1, waiting for transfers between devices, on_device(): right, gram = lax.psum((part_right, own_share), ('dp', 'tp'))  77.7 us
    psum x1, blocking collectives, on_device(): right, gram = lax.psum((part_right, own_share), ('dp', 'tp'))  39.5 us
    psum x1, blocking collectives, on_device(): left = lax.psum(part_left, 'dp')  16.7 us
    dot_general x1, matrix products, on_device(): jnp.einsum('lir,lrw->liw', left, mixed, precision=lax.Precision.HIGHEST)  4.38 us
  transfers between devices with their start and end apart: 1, of which 1 were waited for; matrix products, arithmetic and copies ran while one was open for 4% of the time, Pallas kernels for 0%

commit v1 on v0

--- a/solution.py
+++ b/solution.py
@@ -14,7 +14,8 @@
         right_factor.astype(jnp.bfloat16),
         preferred_element_type=jnp.float32,
     )
-    left = lax.psum(part_left, "dp")
+    blocks = lax.all_gather(part_left, "dp", axis=0, tiled=False)
+    left = blocks.sum(axis=0)
     part_gram = jnp.einsum("lir,lis->lrs", left, left, precision=lax.Precision.HIGHEST)
     small_left = left.astype(jnp.bfloat16)
     part_right = jnp.einsum(

time: 167 us -> 160 us (0.958)
  blocking collectives: 56.2 us -> 48.2 us
    psum x1 -> x0, blocking collectives: 16.7 us -> none  [on_device(): left = lax.psum(part_left, 'dp')]
    all_gather x0 -> x1, blocking collectives: none -> 8.73 us  [on_device(): blocks = lax.all_gather(part_left, 'dp', axis=0, tiled=False)]
where the time goes in v1:
time: 160 us; the launch traced here: 159 us
  waiting for transfers between devices  78.5 us (49%)
  blocking collectives  48.2 us (30%)
  between operations  14.1 us (9%)
  matrix products  8.45 us (5%)
  other arithmetic  7.6 us (5%)
  local copies, waits for them, and re-layouts  2.46 us (2%)
    psum x1, waiting for transfers between devices, on_device(): right, gram = lax.psum((part_right, own_share), ('dp', 'tp'))  78.5 us
    psum x1, blocking collectives, on_device(): right, gram = lax.psum((part_right, own_share), ('dp', 'tp'))  39.5 us
    all_gather x1, blocking collectives, on_device(): blocks = lax.all_gather(part_left, 'dp', axis=0, tiled=False)  8.73 us
    dot_general x1, matrix products, on_device(): jnp.einsum('lir,lrw->liw', left, mixed, precision=lax.Precision.HIGHEST)  4.38 us
  transfers between devices with their start and end apart: 1, of which 1 were waited for; matrix products, arithmetic and copies ran while one was open for 4% of the time, Pallas kernels for 0%

profile of v1, /device:TPU:8, one launch (start us, length us, event | category | flops | bytes accessed | tf_op | source)
XLA Modules:
  0.0 159.4 jit_solution(5869844852154798901)
XLA Ops:
  7.2 0.0 copy-start
  7.2 0.0 all-reduce.2.cloned.1.call-start
  7.2 1.6 %copy-done = bf16[1,4,384,768]{3,2,1,0:T(8,128)(2,1)S(1)} copy-done((bf16[1,4,384,768]{3,2,1,0:T(8,128)(2,1)S(1)}, bf16[1,4,384,768]{3,2,1,0:T(8,128)(2,1)}, u32[]{:S(2)}) %copy-start) | copy-done | bytes 2359320
  8.8 1.6 fusion.2
  10.4 8.7 %all-gather = f32[16,384,8]{1,2,0:T(8,128)S(1)} all-gather(f32[4,384,8]{1,2,0:T(8,128)S(1)} %fusion.2), channel_id=2, replica_groups=mesh['dp'=4,'tp'=8] {'dp'}, dimensions={0}, use_global_device_ids=true | all-gather | bytes 245760 | tf_op jit(solution)/shard_map/all_gather | solution.py:17
  19.2 1.1 fusion.5
  20.2 0.0 all-reduce.2.cloned.1.call-update
  20.3 0.2 convolution_multiply_fusion.1
  20.5 0.1 copy.17
  20.6 39.5 %psum.14 = f32[4,8,8]{1,2,0:T(8,128)S(1)} all-reduce(f32[4,8,8]{1,2,0:T(8,128)S(1)} %convolution_multiply_fusion.1), channel_id=1, replica_groups=mesh['dp'=4,'tp'=8] {'dp','tp'}, use_global_device_ids=true, to_apply=%region_1.0 | all-reduce | flops 256 | bytes 2048 | tf_op jit(solution)/shard_map/psum | solution.py:25
  60.1 0.1 copy.16
  60.2 0.6 gather_fusion
  60.8 0.1 multiply_add_fusion
  60.9 0.1 copy.18
  60.9 0.1 fusion.15
  61.0 2.9 %custom-call.9 = f32[4,8,8]{2,1,0:T(8,128)S(1)} custom-call(f32[4,8,8]{2,1,0:T(8,128)S(1)} %fusion.15), custom_call_target="Cholesky" | custom-call | tf_op jit(solution)/shard_map/jit(cholesky)/cholesky | solution.py:31
  63.9 0.1 select_reduce_fusion
  64.0 0.1 compare_reduce_fusion
  64.1 0.1 select_bitcast_fusion
  64.2 2.5 %custom-call.10 = f32[4,1,8,8]{2,3,1,0:T(8,128)S(1)} custom-call(f32[4,1,8,8]{3,2,1,0:T(8,128)S(1)} %select_bitcast_fusion), custom_call_target="InvertDiagBlocksLowerTriangular" | custom-call | tf_op jit(solution)/shard_map/triangular_solve | solution.py:35
  66.7 78.5 %all-reduce.2.cloned.1.call-done = f32[4,768,8]{1,2,0:T(8,128)} async-done(((f32[4,768,8]{1,2,0:T(8,128)}), f32[4,768,8]{1,2,0:T(8,128)}) %all-reduce.2.cloned.1.call-update) | async-done | bytes 98320 | tf_op jit(solution)/shard_map/psum | solution.py:25
  145.2 1.0 multiply_reduce_fusion
  146.2 1.1 fusion.9
  147.3 0.2 fusion.12
  147.4 0.0 copy-start.1
  147.4 4.4 %multiply_subtract_fusion = (f32[4,384,192]{1,2,0:T(8,128)}, f32[4,384,192]{1,2,0:T(8,128)}) fusion(f32[4,384,192]{1,2,0:T(8,128)} %param.6, f32[4,384,8]{1,2,0:T(8,128)S(1)} %reduce_sum.27, f32[4,8,192]{2,1,0:T(8,128)S(1)} %fusion.12, f32[4,384,192]{1,2,0:T(8,128)} %param.7), kind=kOutput, calls=%fused_computation.7 | convolution fusion | flops 29786112 | bytes 4792320 | tf_op jit(solution)/shard_map/lir,lrw->liw/dot_general | solution.py:36
  151.8 0.0 copy-done.1
  151.8 0.7 broadcast_multiply_fusion
  (8 shorter events, 0.1 us)
Async XLA Ops:
  7.2 1.7 %copy-start = (bf16[1,4,384,768]{3,2,1,0:T(8,128)(2,1)S(1)}, bf16[1,4,384,768]{3,2,1,0:T(8,128)(2,1)}, u32[]{:S(2)}) copy-start(bf16[1,4,384,768]{3,2,1,0:T(8,128)(2,1)} %param.4) | copy-start | bytes 7077892
  7.2 138.0 %all-reduce.2.cloned.1.call-start = ((), (), s32[]{:S(2)}) async-start(), calls=%async_computation | async-start | bytes 196608 | tf_op jit(solution)/shard_map/psum | solution.py:25
  147.4 4.4 %copy-start.1 = (f32[4,768,8]{1,2,0:T(8,128)S(1)}, f32[4,768,8]{1,2,0:T(8,128)}, u32[]{:S(2)}) copy-start(f32[4,768,8]{1,2,0:T(8,128)} %all-reduce.2.cloned.1.call-done) | copy-start | bytes 294916
Sparse Core Ops, SparseCore 0:
  20.4 124.7 all-reduce.1
